TPU v7x, 512 devices: a whole 4x8x8 slice. The times are simulated.
512 devices in a mesh: cfg: 2 (over x_lo), ctx: 32 (over y, x_hi, core), tp: 8 (over z).
Axes of the slice: x: 4 (x_hi: 2, x_lo: 2; x = x_hi * 2 + x_lo), y: 8, z: 8, core: 2. Of those that a mesh axis runs over, the one named last changes fastest.
Arguments:
- query_proj: bfloat16 [2, 8192, 3072], P('cfg', 'ctx', 'tp'), may hold values from -8 to 8
- key_proj: bfloat16 [2, 8192, 3072], P('cfg', 'ctx', 'tp'), may hold values from -8 to 8
- value_proj: bfloat16 [2, 8192, 3072], P('cfg', 'ctx', 'tp'), may hold values from -6 to 6
- query_gain: float32 [128], replicated, may hold values from 1 to 8
- key_gain: float32 [128], replicated, may hold values from 1 to 8
- block_input: bfloat16 [2, 8192, 3072], P('cfg', ('ctx', 'tp')), may hold values from -120 to 120
- cached_out: bfloat16 [2, 8192, 3072], P('cfg', ('ctx', 'tp')), may hold values from -120 to 120
- replay_mask: int32 [2, 8192], P('cfg', 'ctx'), may hold values from 0 to 1, as said below
- branch_gate: float32 [2, 3072], P('cfg'), may hold values from 1 to 4
- attn_weight: bfloat16 [3072, 3072], P('tp'), may hold values from -0.109375 to 0.109375
- final_shift: float32 [2, 3072], P('cfg'), may hold values from -4 to 4
- final_scale: float32 [2, 3072], P('cfg'), may hold values from -2 to 2
- patch_weight: bfloat16 [3072, 64], replicated, may hold values from -0.109375 to 0.109375
Outputs:
- block_out: bfloat16 [2, 8192, 3072], P('cfg', ('ctx', 'tp'))
- velocity: float32 [8192, 64], P(('ctx', 'tp'), 'cfg')
Inputs may be any that keep to these rules, and one draw needn't show every extreme that they name: `replay_mask`: in each branch, at most 128 of the 256 rows of one index of ctx have a 0, and some index of ctx has exactly 128.
All inputs are finite; a program needn't handle non-finite values.
Results may differ from a plain program's by a relative error of at most 0.0097.
Values may be sent and summed in bfloat16 or wider, within the bound.
A program may use at most 128 MiB of HBM per device.

v0:
```python
import jax
import jax.numpy as jnp
from jax import lax
from jax.sharding import PartitionSpec as P

guidance_scale = 3.0


def sent_together(arrays, axis, dim, along):
    widths = [a.shape[along] for a in arrays]
    both = jnp.concatenate(arrays, axis=along)
    filled = lax.all_gather(both, axis, axis=dim, tiled=True)
    return tuple(jnp.split(filled, [sum(widths[:k]) for k in range(1, len(widths))], axis=along))


def norm_heads(values, gain):
    width = values.shape[-1]
    depth = gain.shape[0]
    lifted = values.astype(jnp.float32).reshape(values.shape[:-1] + (width // depth, depth))
    mean_square = jnp.mean(lifted * lifted, axis=-1, keepdims=True)
    scaled = lifted * lax.rsqrt(mean_square + 1e-06) * gain
    return scaled.reshape(values.shape).astype(jnp.bfloat16)


def absorb(state, keys_part, values_part, query_heads):
    heads = query_heads.shape[0]
    depth = query_heads.shape[2]
    length = keys_part.shape[0]
    block = 512
    key_blocks = keys_part.reshape(length // block, block, heads, depth)
    value_blocks = values_part.reshape(length // block, block, heads, depth)
    scale = depth ** (-0.5)

    def update(carried, blocks):
        summed, biggest, totals = carried
        keys_here, values_here = blocks
        scores = (
            jnp.einsum("hqd,khd->hqk", query_heads, keys_here, preferred_element_type=jnp.float32)
            * scale
        )
        newest = jnp.maximum(biggest, jnp.max(scores, axis=-1))
        factor = jnp.exp(biggest - newest)
        weights = jnp.exp(scores - newest[..., None])
        totals = totals * factor + jnp.sum(weights, axis=-1)
        added = jnp.einsum(
            "hqk,khd->hqd",
            weights.astype(jnp.bfloat16),
            values_here,
            preferred_element_type=jnp.float32,
        )
        summed = summed * factor[..., None] + added
        return ((summed, newest, totals), None)

    state, unused = lax.scan(update, state, (key_blocks, value_blocks))
    return state


def shards(
    query_proj,
    key_proj,
    value_proj,
    query_gain,
    key_gain,
    block_input,
    cached_out,
    replay_mask,
    branch_gate,
    attn_weight,
    final_shift,
    final_scale,
    patch_weight,
):
    count = query_proj.shape[1]
    width = query_proj.shape[2]
    depth = query_gain.shape[0]
    heads = width // depth
    live_count = count // 2
    share = count // lax.axis_size("tp")
    queries = norm_heads(query_proj[0], query_gain)
    keys_normed = norm_heads(key_proj[0], key_gain)
    values_local = value_proj[0]
    mask_local = replay_mask[0]
    selected = jnp.argsort(mask_local, stable=True)[:live_count]
    picked = queries[selected]
    picked_count = picked.shape[0]
    query_heads = picked.reshape(picked_count, heads, depth).transpose(1, 0, 2)
    start_state = (
        jnp.zeros((heads, picked_count, depth), jnp.float32),
        jnp.full((heads, picked_count), -1e30, jnp.float32),
        jnp.zeros((heads, picked_count), jnp.float32),
    )
    piece = sent_together((keys_normed, values_local), "ctx", 0, 1)
    state = absorb(start_state, piece[0], piece[1], query_heads)
    summed, biggest, totals = state
    attended_picked = (
        (summed / totals[..., None])
        .transpose(1, 0, 2)
        .reshape(picked_count, width)
        .astype(jnp.bfloat16)
    )
    attended = jnp.zeros((count, width), jnp.bfloat16).at[selected].set(attended_picked)
    projected = lax.psum_scatter(
        jnp.dot(attended, attn_weight, preferred_element_type=jnp.float32).astype(jnp.bfloat16),
        "tp",
        scatter_dimension=0,
        tiled=True,
    ).astype(jnp.float32)
    mask_rows = lax.dynamic_slice_in_dim(mask_local, lax.axis_index("tp") * share, share, 0)
    mixed = block_input[0].astype(jnp.float32) + branch_gate[0][None, :] * projected
    block_out = jnp.where(mask_rows[:, None] == 1, cached_out[0].astype(jnp.float32), mixed).astype(
        jnp.bfloat16
    )
    lifted = block_out.astype(jnp.float32)
    center = jnp.mean(lifted, axis=-1, keepdims=True)
    spread = jnp.mean((lifted - center) * (lifted - center), axis=-1, keepdims=True)
    normed = (
        (lifted - center) * lax.rsqrt(spread + 1e-06) * (1.0 + final_scale[0][None, :])
        + final_shift[0][None, :]
    ).astype(jnp.bfloat16)
    branch_out = jnp.dot(normed, patch_weight, preferred_element_type=jnp.float32)
    paired = lax.all_to_all(branch_out, "cfg", split_axis=1, concat_axis=0, tiled=True)
    cond_part = paired[:share]
    uncond_part = paired[share:]
    velocity = uncond_part + guidance_scale * (cond_part - uncond_part)
    return (block_out[None], velocity)


def solution(mesh):
    in_specs = (
        P("cfg", "ctx", "tp"),
        P("cfg", "ctx", "tp"),
        P("cfg", "ctx", "tp"),
        P(),
        P(),
        P("cfg", ("ctx", "tp"), None),
        P("cfg", ("ctx", "tp"), None),
        P("cfg", "ctx"),
        P("cfg", None),
        P("tp", None),
        P("cfg", None),
        P("cfg", None),
        P(),
    )
    out_specs = (P("cfg", ("ctx", "tp"), None), P(("ctx", "tp"), "cfg"))
    return jax.shard_map(shards, mesh=mesh, in_specs=in_specs, out_specs=out_specs, check_vma=False)
```

profile of v0, /device:TPU:8, one launch (start us, length us, event | category | flops | bytes accessed | tf_op | source)
XLA Modules:
  0.0 299.3 jit_solution(18116649159860371368)
XLA Ops:
  14.5 3.2 %sort.17 = (s32[256]{0:T(256)}, s32[256]{0:T(256)S(1)}) sort(s32[256]{0:T(256)S(1)} %bitcast.110, s32[256]{0:T(256)S(1)} %iota.4), dimensions={0}, to_apply=%region_0.0 | sort | flops 2048 | bytes 4096 | tf_op jit(solution)/shard_map/jit(argsort)/sort | solution.py:83
  19.4 131.4 %all-gather.2.cloned.1.call-done = bf16[8192,768]{0,1:T(8,128)(2,1)} async-done(((bf16[256,768]{0,1:T(8,128)(2,1)}), bf16[8192,768]{0,1:T(8,128)(2,1)}) %all-gather.2.cloned.1.call-update) | async-done | bytes 12582928 | tf_op jit(solution)/shard_map/all_gather | solution.py:12
  150.8 8.2 %fusion.39 = (bf16[8192,384]{0,1:T(8,128)(2,1)}, bf16[8192,384]{0,1:T(8,128)(2,1)S(1)}) fusion(bf16[8192,768]{0,1:T(8,128)(2,1)} %all-gather.2.cloned.1.call-done), kind=kLoop, calls=%fused_computation.67 | loop fusion | bytes 25165824 | tf_op jit(solution)/shard_map/split | solution.py:13
  159.0 5.6 %copy.42 = bf16[48,8,16,512]{3,2,1,0:T(8,128)(2,1)} copy(bf16[48,8,16,512]{3,1,2,0:T(8,128)(2,1)S(1)} %bitcast.99) | data formatting | bytes 12582912
  164.6 9.1 %copy.35 = bf16[16,512,3,128]{3,1,2,0:T(8,128)(2,1)} copy(bf16[16,512,3,128]{1,0,3,2:T(8,128)(2,1)} %bitcast.96) | data formatting | bytes 12582912
  173.7 8.3 %copy.43 = bf16[48,8,16,512]{3,2,1,0:T(8,128)(2,1)} copy(bf16[48,8,16,512]{3,1,2,0:T(8,128)(2,1)} %bitcast.98) | data formatting | bytes 12582912
  182.0 9.2 %copy.37 = bf16[16,512,3,128]{3,1,2,0:T(8,128)(2,1)} copy(bf16[16,512,3,128]{1,0,3,2:T(8,128)(2,1)} %bitcast.97) | data formatting | bytes 12582912
  191.2 45.7 %while.15 = (s32[]{:T(128)}, f32[3,128,128]{2,1,0:T(8,128)S(1)}, f32[3,128]{1,0:T(4,128)S(1)}, f32[3,128]{1,0:T(4,128)S(1)}, bf16[16,512,3,128]{3,1,2,0:T(8,128)...) while((s32[]{:T(128)}, f32[3,128,128]{2,1,0:T(8,128)S(1)}, ...), condition=%wide.region_6.7_spmd.clone, body=%wide.region_3.6_spmd.clone.sunk | while | flops 101992320 | bytes 3662953 | solution.py:54
  192.6 1.4 convolution_add_fusion.2
  194.0 1.3 fusion.53
  195.5 1.4 convolution_add_fusion.2
  198.3 1.4 convolution_add_fusion.2
  201.2 1.4 convolution_add_fusion.2
  204.1 1.4 convolution_add_fusion.2
  205.5 1.3 fusion.53
  206.9 1.4 convolution_add_fusion.2
  209.8 1.4 convolution_add_fusion.2
  211.2 1.3 fusion.53
  212.6 1.4 convolution_add_fusion.2
  215.5 1.4 convolution_add_fusion.2
  218.3 1.4 convolution_add_fusion.2
  221.2 1.4 convolution_add_fusion.2
  222.6 1.3 fusion.53
  224.0 1.4 convolution_add_fusion.2
  226.9 1.4 convolution_add_fusion.2
  229.7 1.4 convolution_add_fusion.2
  232.6 1.4 convolution_add_fusion.2
  235.5 1.4 convolution_add_fusion.2
  238.5 2.1 convolution_convert_fusion
  240.7 40.6 %reduce-scatter.2.cloned.1.call-done = bf16[32,3072]{1,0:T(8,128)(2,1)} async-done(((bf16[256,3072]{1,0:T(8,128)(2,1)}), bf16[32,3072]{1,0:T(8,128)(2,1)}) %reduce-scatter.2.cloned.1.call-update) | async-done | bytes 196624 | tf_op jit(solution)/shard_map/reduce_scatter | solution.py:102
  282.7 1.3 fusion.26
  284.2 6.3 %all_to_all.16 = f32[2,1,1024]{2,1,0:T(1,128)S(1)} all-to-all(f32[2,1,1024]{2,1,0:T(1,128)S(1)} %reshape.115), channel_id=1, replica_groups=mesh['cfg'=2,'ctx'=32,'tp'=8] {'cfg'}, dimensions={0} | all-to-all | bytes 16384 | tf_op jit(solution)/shard_map/all_to_all | solution.py:121
  (145 shorter events, 31.8 us)
Async XLA Ops:
  7.2 231.3 %copy-start = (bf16[384,3072]{1,0:T(8,128)(2,1)S(1)}, bf16[384,3072]{1,0:T(8,128)(2,1)}, u32[]{:S(2)}) copy-start(bf16[384,3072]{1,0:T(8,128)(2,1)} %param.24) | copy-start | bytes 7077892
  7.2 11.0 %copy-start.2 = (bf16[1,256,384]{2,1,0:T(8,128)(2,1)S(1)}, bf16[1,256,384]{2,1,0:T(8,128)(2,1)}, u32[]{:S(2)}) copy-start(bf16[1,256,384]{2,1,0:T(8,128)(2,1)} %param.15) | copy-start | bytes 589828
  7.2 7.3 %copy-start.7 = (s32[1,256]{1,0:T(1,128)S(1)}, s32[1,256]{1,0:T(1,128)}, u32[]{:S(2)}) copy-start(s32[1,256]{1,0:T(1,128)} %param.22) | copy-start | bytes 3076
  7.2 11.0 %copy-start.8 = (f32[128]{0:T(128)S(1)}, f32[128]{0:T(128)}, u32[]{:S(2)}) copy-start(f32[128]{0:T(128)} %param.18) | copy-start | bytes 1540
  7.2 143.6 %all-gather.2.cloned.1.call-start = ((), (), s32[]{:S(2)}) async-start(), calls=%async_computation.2 | async-start | bytes 12976128 | tf_op jit(solution)/shard_map/all_gather | solution.py:12
  11.2 270.1 %reduce-scatter.2.cloned.1.call-start = ((), (), s32[]{:S(2)}) async-start(), calls=%async_computation.3 | async-start | bytes 1769472 | tf_op jit(solution)/shard_map/reduce_scatter | solution.py:102
  17.7 0.5 copy-start.9
  236.9 3.8 %copy-start.5 = (f32[1,3072]{1,0:T(1,128)S(1)}, f32[1,3072]{1,0:T(1,128)}, u32[]{:S(2)}) copy-start(f32[1,3072]{1,0:T(1,128)} %param.26) | copy-start | bytes 36868
  236.9 44.5 %copy-start.3 = (bf16[1,32,3072]{2,1,0:T(8,128)(2,1)S(1)}, bf16[1,32,3072]{2,1,0:T(8,128)(2,1)}, u32[]{:S(2)}) copy-start(bf16[1,32,3072]{2,1,0:T(8,128)(2,1)} %param.20) | copy-start | bytes 589828
  236.9 44.4 %copy-start.4 = (bf16[1,32,3072]{2,1,0:T(8,128)(2,1)S(1)}, bf16[1,32,3072]{2,1,0:T(8,128)(2,1)}, u32[]{:S(2)}) copy-start(bf16[1,32,3072]{2,1,0:T(8,128)(2,1)} %param.21) | copy-start | bytes 589828
  236.9 44.4 %copy-start.6 = (f32[1,3072]{1,0:T(1,128)S(1)}, f32[1,3072]{1,0:T(1,128)}, u32[]{:S(2)}) copy-start(f32[1,3072]{1,0:T(1,128)} %param.23) | copy-start | bytes 36868
  236.9 45.8 %copy-start.10 = (f32[1,3072]{1,0:T(1,128)S(1)}, f32[1,3072]{1,0:T(1,128)}, u32[]{:S(2)}) copy-start(f32[1,3072]{1,0:T(1,128)} %param.25) | copy-start | bytes 36868
  282.5 10.0 %copy-start.1 = (bf16[32,3072]{1,0:T(8,128)(2,1)}, bf16[32,3072]{1,0:T(8,128)(2,1)S(1)}, u32[]{:S(2)}) copy-start(bf16[32,3072]{1,0:T(8,128)(2,1)S(1)} %get-tuple-element.99) | copy-start | bytes 589828
Sparse Core Ops, SparseCore 0:
  11.4 139.4 all-gather.1
  240.7 40.5 reduce-scatter.1
where the time goes:
time: 301 us; the launch traced here: 299 us
  waiting for transfers between devices  172 us (57%)
  local copies, waits for them, and re-layouts  49.4 us (16%)
  matrix products  45.9 us (15%)
  between operations  14.3 us (5%)
  other arithmetic  10.4 us (3%)
  blocking collectives  6.35 us (2%)
    all_gather x1, waiting for transfers between devices, sent_together(): filled = lax.all_gather(both, axis, axis=dim, tiled=True)  131 us
    reduce_scatter x1, waiting for transfers between devices, shards(): lax.psum_scatter(jnp.dot(attended, attn_weight, preferred_element_type=jn...  40.6 us
    unnamed x31, local copies, waits for them, and re-layouts  35.3 us
    dot_general x16, matrix products, update(): jnp.einsum('hqk,khd->hqd', weights.astype(jnp.bfloat16), values_here, pre...  22 us
    dot_general x16, matrix products, update(): jnp.einsum('hqd,khd->hqk', query_heads, keys_here, preferred_element_type...  20.5 us
    split x1, local copies, waits for them, and re-layouts, sent_together(): jnp.split(filled, [sum(widths[:k]) for k in range(1, len(widths))], axis=...  8.21 us
    all_to_all x1, blocking collectives, shards(): lax.all_to_all(branch_out, 'cfg', split_axis=1, concat_axis=0, tiled=True)  6.35 us
  transfers between devices with their start and end apart: 2, of which 2 were waited for; matrix products, arithmetic and copies ran while one was open for 3% of the time, Pallas kernels for 0%

commit v1 on v0

--- a/solution.py
+++ b/solution.py
@@ -118,7 +118,10 @@
         + final_shift[0][None, :]
     ).astype(jnp.bfloat16)
     branch_out = jnp.dot(normed, patch_weight, preferred_element_type=jnp.float32)
-    paired = lax.all_to_all(branch_out, "cfg", split_axis=1, concat_axis=0, tiled=True)
+    paired = jnp.concatenate(
+        lax.all_to_all(jnp.stack(jnp.split(branch_out, lax.axis_size("cfg"), axis=1)), "cfg", 0, 0),
+        axis=0,
+    )
     cond_part = paired[:share]
     uncond_part = paired[share:]
     velocity = uncond_part + guidance_scale * (cond_part - uncond_part)

time: 301 us -> 301 us (level)
  no operation moved by 1% of the time
where the time goes in v1:
time: 301 us; the launch traced here: 299 us
  waiting for transfers between devices  172 us (57%)
  local copies, waits for them, and re-layouts  49.4 us (16%)
  matrix products  45.9 us (15%)
  between operations  14.3 us (5%)
  other arithmetic  10.5 us (3%)
  blocking collectives  6.35 us (2%)
    all_gather x1, waiting for transfers between devices, sent_together(): filled = lax.all_gather(both, axis, axis=dim, tiled=True)  131 us
    reduce_scatter x1, waiting for transfers between devices, shards(): lax.psum_scatter(jnp.dot(attended, attn_weight, preferred_element_type=jn...  40.6 us
    unnamed x31, local copies, waits for them, and re-layouts  35.3 us
    dot_general x16, matrix products, update(): jnp.einsum('hqk,khd->hqd', weights.astype(jnp.bfloat16), values_here, pre...  22 us
    dot_general x16, matrix products, update(): jnp.einsum('hqd,khd->hqk', query_heads, keys_here, preferred_element_type...  20.5 us
    split x1, local copies, waits for them, and re-layouts, sent_together(): jnp.split(filled, [sum(widths[:k]) for k in range(1, len(widths))], axis=...  8.21 us
    all_to_all x1, blocking collectives, shards(): lax.all_to_all(jnp.stack(jnp.split(branch_out, lax.axis_size('cfg'), axis...  6.35 us
  transfers between devices with their start and end apart: 2, of which 2 were waited for; matrix products, arithmetic and copies ran while one was open for 3% of the time, Pallas kernels for 0%

profile of v1, /device:TPU:8, one launch (start us, length us, event | category | flops | bytes accessed | tf_op | source)
XLA Modules:
  0.0 299.3 jit_solution(3516769743607256806)
XLA Ops:
  14.5 3.2 %sort.17 = (s32[256]{0:T(256)}, s32[256]{0:T(256)S(1)}) sort(s32[256]{0:T(256)S(1)} %bitcast.106, s32[256]{0:T(256)S(1)} %iota.4), dimensions={0}, to_apply=%region_0.0 | sort | flops 2048 | bytes 4096 | tf_op jit(solution)/shard_map/jit(argsort)/sort | solution.py:83
  19.4 131.4 %all-gather.2.cloned.1.call-done = bf16[8192,768]{0,1:T(8,128)(2,1)} async-done(((bf16[256,768]{0,1:T(8,128)(2,1)}), bf16[8192,768]{0,1:T(8,128)(2,1)}) %all-gather.2.cloned.1.call-update) | async-done | bytes 12582928 | tf_op jit(solution)/shard_map/all_gather | solution.py:12
  150.8 8.2 %fusion.39 = (bf16[8192,384]{0,1:T(8,128)(2,1)}, bf16[8192,384]{0,1:T(8,128)(2,1)S(1)}) fusion(bf16[8192,768]{0,1:T(8,128)(2,1)} %all-gather.2.cloned.1.call-done), kind=kLoop, calls=%fused_computation.70 | loop fusion | bytes 25165824 | tf_op jit(solution)/shard_map/split | solution.py:13
  159.0 5.6 %copy.39 = bf16[48,8,16,512]{3,2,1,0:T(8,128)(2,1)} copy(bf16[48,8,16,512]{3,1,2,0:T(8,128)(2,1)S(1)} %bitcast.96) | data formatting | bytes 12582912
  164.6 9.1 %copy.33 = bf16[16,512,3,128]{3,1,2,0:T(8,128)(2,1)} copy(bf16[16,512,3,128]{1,0,3,2:T(8,128)(2,1)} %bitcast.93) | data formatting | bytes 12582912
  173.7 8.3 %copy.40 = bf16[48,8,16,512]{3,2,1,0:T(8,128)(2,1)} copy(bf16[48,8,16,512]{3,1,2,0:T(8,128)(2,1)} %bitcast.95) | data formatting | bytes 12582912
  182.0 9.2 %copy.35 = bf16[16,512,3,128]{3,1,2,0:T(8,128)(2,1)} copy(bf16[16,512,3,128]{1,0,3,2:T(8,128)(2,1)} %bitcast.94) | data formatting | bytes 12582912
  191.2 45.7 %while.15 = (s32[]{:T(128)}, f32[3,128,128]{2,1,0:T(8,128)S(1)}, f32[3,128]{1,0:T(4,128)S(1)}, f32[3,128]{1,0:T(4,128)S(1)}, bf16[16,512,3,128]{3,1,2,0:T(8,128)...) while((s32[]{:T(128)}, f32[3,128,128]{2,1,0:T(8,128)S(1)}, ...), condition=%wide.region_6.7_spmd.clone, body=%wide.region_3.6_spmd.clone.sunk | while | flops 101992320 | bytes 3662953 | solution.py:54
  192.6 1.4 convolution_add_fusion.2
  194.0 1.3 fusion.53
  195.5 1.4 convolution_add_fusion.2
  198.3 1.4 convolution_add_fusion.2
  201.2 1.4 convolution_add_fusion.2
  204.1 1.4 convolution_add_fusion.2
  205.5 1.3 fusion.53
  206.9 1.4 convolution_add_fusion.2
  209.8 1.4 convolution_add_fusion.2
  211.2 1.3 fusion.53
  212.6 1.4 convolution_add_fusion.2
  215.5 1.4 convolution_add_fusion.2
  218.3 1.4 convolution_add_fusion.2
  221.2 1.4 convolution_add_fusion.2
  222.6 1.3 fusion.53
  224.0 1.4 convolution_add_fusion.2
  226.9 1.4 convolution_add_fusion.2
  229.7 1.4 convolution_add_fusion.2
  232.6 1.4 convolution_add_fusion.2
  235.5 1.4 convolution_add_fusion.2
  238.5 2.1 convolution_convert_fusion
  240.7 40.6 %reduce-scatter.2.cloned.1.call-done = bf16[32,3072]{1,0:T(8,128)(2,1)} async-done(((bf16[256,3072]{1,0:T(8,128)(2,1)}), bf16[32,3072]{1,0:T(8,128)(2,1)}) %reduce-scatter.2.cloned.1.call-update) | async-done | bytes 196624 | tf_op jit(solution)/shard_map/reduce_scatter | solution.py:102
  282.7 1.3 fusion.26
  284.2 6.3 %all_to_all.5 = f32[2,1,1024]{2,1,0:T(1,128)S(1)} all-to-all(f32[2,1,1024]{2,1,0:T(1,128)S(1)} %reshape.113), channel_id=1, replica_groups=mesh['cfg'=2,'ctx'=32,'tp'=8] {'cfg'}, dimensions={0} | all-to-all | bytes 16384 | tf_op jit(solution)/shard_map/all_to_all | solution.py:122
  (144 shorter events, 31.8 us)
Async XLA Ops:
  7.2 231.3 %copy-start = (bf16[384,3072]{1,0:T(8,128)(2,1)S(1)}, bf16[384,3072]{1,0:T(8,128)(2,1)}, u32[]{:S(2)}) copy-start(bf16[384,3072]{1,0:T(8,128)(2,1)} %param.24) | copy-start | bytes 7077892
  7.2 11.0 %copy-start.2 = (bf16[1,256,384]{2,1,0:T(8,128)(2,1)S(1)}, bf16[1,256,384]{2,1,0:T(8,128)(2,1)}, u32[]{:S(2)}) copy-start(bf16[1,256,384]{2,1,0:T(8,128)(2,1)} %param.15) | copy-start | bytes 589828
  7.2 7.3 %copy-start.7 = (s32[1,256]{1,0:T(1,128)S(1)}, s32[1,256]{1,0:T(1,128)}, u32[]{:S(2)}) copy-start(s32[1,256]{1,0:T(1,128)} %param.22) | copy-start | bytes 3076
  7.2 11.0 %copy-start.8 = (f32[128]{0:T(128)S(1)}, f32[128]{0:T(128)}, u32[]{:S(2)}) copy-start(f32[128]{0:T(128)} %param.18) | copy-start | bytes 1540
  7.2 143.6 %all-gather.2.cloned.1.call-start = ((), (), s32[]{:S(2)}) async-start(), calls=%async_computation.2 | async-start | bytes 12976128 | tf_op jit(solution)/shard_map/all_gather | solution.py:12
  11.2 270.1 %reduce-scatter.2.cloned.1.call-start = ((), (), s32[]{:S(2)}) async-start(), calls=%async_computation.3 | async-start | bytes 1769472 | tf_op jit(solution)/shard_map/reduce_scatter | solution.py:102
  17.7 0.5 copy-start.9
  236.9 3.8 %copy-start.5 = (f32[1,3072]{1,0:T(1,128)S(1)}, f32[1,3072]{1,0:T(1,128)}, u32[]{:S(2)}) copy-start(f32[1,3072]{1,0:T(1,128)} %param.26) | copy-start | bytes 36868
  236.9 44.5 %copy-start.3 = (bf16[1,32,3072]{2,1,0:T(8,128)(2,1)S(1)}, bf16[1,32,3072]{2,1,0:T(8,128)(2,1)}, u32[]{:S(2)}) copy-start(bf16[1,32,3072]{2,1,0:T(8,128)(2,1)} %param.20) | copy-start | bytes 589828
  236.9 44.4 %copy-start.4 = (bf16[1,32,3072]{2,1,0:T(8,128)(2,1)S(1)}, bf16[1,32,3072]{2,1,0:T(8,128)(2,1)}, u32[]{:S(2)}) copy-start(bf16[1,32,3072]{2,1,0:T(8,128)(2,1)} %param.21) | copy-start | bytes 589828
  236.9 44.4 %copy-start.6 = (f32[1,3072]{1,0:T(1,128)S(1)}, f32[1,3072]{1,0:T(1,128)}, u32[]{:S(2)}) copy-start(f32[1,3072]{1,0:T(1,128)} %param.23) | copy-start | bytes 36868
  236.9 45.8 %copy-start.10 = (f32[1,3072]{1,0:T(1,128)S(1)}, f32[1,3072]{1,0:T(1,128)}, u32[]{:S(2)}) copy-start(f32[1,3072]{1,0:T(1,128)} %param.25) | copy-start | bytes 36868
  282.5 10.0 %copy-start.1 = (bf16[32,3072]{1,0:T(8,128)(2,1)}, bf16[32,3072]{1,0:T(8,128)(2,1)S(1)}, u32[]{:S(2)}) copy-start(bf16[32,3072]{1,0:T(8,128)(2,1)S(1)} %get-tuple-element.99) | copy-start | bytes 589828
Sparse Core Ops, SparseCore 0:
  11.4 139.4 all-gather.1
  240.7 40.5 reduce-scatter.1
